TPU v7x, 512 devices: a 8x2x16 block of a 8x16x16 slice. The times are simulated.
512 devices in a mesh: rep: 2 (over y), blk: 128 (over z, x), head: 2 (over core).
Axes of the slice: x: 8, y: 2, z: 16, core: 2. Of those that a mesh axis runs over, the one named last changes fastest.
The devices are a block of a 8x16x16 slice.
Arguments:
- queries: bfloat16 [2, 8192, 8192], P('rep', 'blk', 'head'), parts along dimension 0, may hold values from -200 to 200
- keys: bfloat16 [2, 8192, 512], P('rep', 'blk', 'head'), parts along dimension 0, may hold values from -6 to 6
- values: bfloat16 [2, 8192, 512], P('rep', 'blk', 'head'), parts along dimension 0, may hold values from -6 to 6
- prompt_length: int32 [2], P('rep'), parts along dimension 0, may hold values from 4096 to 8192
- span_order: int32 [512], P('rep'), parts along dimension 0, may hold values from 0 to 255, as said below
Outputs:
- attended: bfloat16 [2, 8192, 8192], P('rep', 'blk', 'head'), parts along dimension 0
There are 2 independent parts, one for each index of `rep`. A program takes and returns all parts, laid end to end along the dimension named above; each array names one. Nothing has to cross between parts.
Inputs may be any that keep to these rules, and one draw needn't show every extreme that they name: `span_order`: each of the 256 span numbers stands in exactly one slot.
All inputs are finite; a program needn't handle non-finite values.
Results may differ from a plain program's by a relative error of at most 0.0065.
Values may be sent and summed in bfloat16 or wider, within the bound.
No kernel may reach another device: no remote copies, remote signals or barrier semaphores. Data moves between devices by JAX's collectives and lax.ppermute only.
A program may use at most 64 MiB of HBM per device.

v0:
```python
import jax
import jax.numpy as jnp
from jax import lax
from jax.sharding import Mesh
from jax.sharding import PartitionSpec as P

HEAD_WIDTH = 128
BLK = ("blk_0", "blk_1")


NEG_FILL = -1e30


def laid_out(pieces, dim):
    pieces = jnp.moveaxis(pieces, 0, dim)
    shape = pieces.shape
    return pieces.reshape(*shape[:dim], shape[dim] * shape[dim + 1], *shape[dim + 2 :])


def stacked_from(value, axes, sequence):
    pieces = value[None]
    for k in sequence:
        pieces = lax.all_gather(pieces, axes[k], axis=0, tiled=True)
    carried = [lax.axis_size(axes[k]) for k in reversed(sequence)]
    pieces = pieces.reshape(*carried, *value.shape)
    turned = sorted(range(len(sequence)), key=lambda place: sequence[len(sequence) - 1 - place])
    return pieces.transpose(*turned, *range(len(sequence), pieces.ndim)).reshape(-1, *value.shape)


def whole_of(value, axes, sequence, dim):
    return laid_out(stacked_from(value, axes, sequence), dim)


def shards(queries, keys, values, prompt_length, span_order):
    mine = lax.axis_index(BLK)
    prompts = queries.shape[0]
    tok_rows = queries.shape[1]
    span = tok_rows // 2
    local_heads = keys.shape[2] // HEAD_WIDTH
    group = queries.shape[2] // (local_heads * HEAD_WIDTH)
    offsets = jnp.arange(span, dtype=jnp.int32)
    all_pos = (span_order[:, None] * span + offsets[None, :]).reshape(-1)
    my_pos = lax.dynamic_slice_in_dim(all_pos, mine * tok_rows, tok_rows)
    row_pos = jnp.tile(my_pos, group)
    q_cols = (
        queries.reshape(prompts, tok_rows, local_heads, group, HEAD_WIDTH)
        .transpose(0, 2, 4, 3, 1)
        .reshape(prompts, local_heads, HEAD_WIDTH, group * tok_rows)
    )
    scale = HEAD_WIDTH ** (-0.5)

    def attend(carry, key_rows, value_rows, key_pos):
        best, total, accum = carry
        count = key_rows.shape[1]
        key_four = key_rows.reshape(prompts, count, local_heads, HEAD_WIDTH)
        value_four = value_rows.reshape(prompts, count, local_heads, HEAD_WIDTH)
        scores = (
            jnp.einsum("skhd,shdr->shkr", key_four, q_cols, preferred_element_type=jnp.float32)
            * scale
        )
        allowed = (key_pos[None, :, None] <= row_pos[None, None, :]) & (
            key_pos[None, :, None] < prompt_length[:, None, None]
        )
        scores = jnp.where(allowed[:, None], scores, NEG_FILL)
        fresh = jnp.maximum(best, jnp.max(scores, axis=2))
        weights = jnp.where(allowed[:, None], jnp.exp(scores - fresh[:, :, None, :]), 0.0)
        factor = jnp.exp(best - fresh)
        total = total * factor + jnp.sum(weights, axis=2)
        mixed = jnp.einsum(
            "shkr,skhd->shrd",
            weights.astype(jnp.bfloat16),
            value_four,
            preferred_element_type=jnp.float32,
        )
        accum = accum * factor[..., None] + mixed
        return (fresh, total, accum)

    def visit(carry, key_rows, value_rows, key_pos):
        return attend(carry, key_rows, value_rows, key_pos)

    def fold_piece(carry, pieces):
        key_rows, value_rows = pieces
        rows = key_rows.shape[1]
        size = max((d for d in range(1, min(rows, 256) + 1) if rows % d == 0))
        steps = rows // size
        if steps == 1:
            return visit(carry, key_rows, value_rows, all_pos)

        def one_block(index, state):
            begin = (index * size).astype(jnp.int32)
            return visit(
                state,
                lax.dynamic_slice_in_dim(key_rows, begin, size, 1),
                lax.dynamic_slice_in_dim(value_rows, begin, size, 1),
                lax.dynamic_slice_in_dim(all_pos, begin, size),
            )

        return lax.fori_loop(0, steps, one_block, carry)

    width = group * tok_rows
    init = (
        jnp.full((prompts, local_heads, width), NEG_FILL, jnp.float32),
        jnp.zeros((prompts, local_heads, width), jnp.float32),
        jnp.zeros((prompts, local_heads, width, HEAD_WIDTH), jnp.float32),
    )
    carry = fold_piece(init, (whole_of(keys, BLK, (0, 1), 1), whole_of(values, BLK, (0, 1), 1)))
    best, total, accum = carry
    normed = accum / total[..., None]
    joined_heads = (
        normed.reshape(prompts, local_heads, group, tok_rows, HEAD_WIDTH)
        .transpose(0, 3, 1, 2, 4)
        .reshape(prompts, tok_rows, local_heads * group * HEAD_WIDTH)
    )
    joined_heads = jnp.where(
        (my_pos[None, :] < prompt_length[:, None])[:, :, None], joined_heads, 0.0
    )
    return joined_heads.astype(jnp.bfloat16)


def solution(mesh):
    split = Mesh(
        mesh.devices.reshape(mesh.shape["rep"], 16, 8, mesh.shape["head"]),
        ("rep", "blk_0", "blk_1", "head"),
    )
    in_specs = (
        P("rep", BLK, "head"),
        P("rep", BLK, "head"),
        P("rep", BLK, "head"),
        P("rep"),
        P("rep"),
    )
    out_specs = P("rep", BLK, "head")
    return jax.shard_map(
        shards, mesh=split, in_specs=in_specs, out_specs=out_specs, check_vma=False
    )
```

profile of v0, /device:TPU:80, one launch (start us, length us, event | category | flops | bytes accessed | tf_op | source)
XLA Modules:
  0.0 428.9 jit_solution(16120057133728882408)
XLA Ops:
  6.6 73.6 %all-gather = bf16[16,64,256]{2,1,0:T(8,128)(2,1)} all-gather(bf16[1,64,256]{2,1,0:T(8,128)(2,1)} %param.8), channel_id=2, replica_groups=mesh['rep'=2,'blk_0'=16,'blk_1'=8,'head'=2] {'blk_0'}, dimensions={0}, use_global_device_ids=true | all-gather | bytes 557056 | tf_op jit(solution)/shard_map/all_gather | solution.py:23
  80.3 31.7 %all-gather.2 = bf16[16,64,256]{2,1,0:T(8,128)(2,1)} all-gather(bf16[1,64,256]{2,1,0:T(8,128)(2,1)} %param.9), channel_id=4, replica_groups=mesh['rep'=2,'blk_0'=16,'blk_1'=8,'head'=2] {'blk_0'}, dimensions={0}, use_global_device_ids=true | all-gather | bytes 557056 | tf_op jit(solution)/shard_map/all_gather | solution.py:23
  113.6 19.8 %all-gather.7.cloned.1.call-done = bf16[128,64,256]{2,1,0:T(8,128)(2,1)} async-done(((bf16[16,64,256]{2,1,0:T(8,128)(2,1)}), bf16[128,64,256]{2,1,0:T(8,128)(2,1)}) %all-gather.7.cloned.1.call-update) | async-done | bytes 4194320 | tf_op jit(solution)/shard_map/all_gather | solution.py:23
  133.4 4.7 %copy.39 = bf16[16,8,1,64,256]{4,3,1,0,2:T(8,128)(2,1)} copy(bf16[16,8,1,64,256]{4,3,0,1,2:T(8,128)(2,1)} %bitcast.69) | data formatting | bytes 8388608 | tf_op jit(solution)/shard_map/transpose | solution.py:27
  138.1 57.4 %all-gather.9.cloned.1.call-done = bf16[128,64,256]{2,1,0:T(8,128)(2,1)} async-done(((bf16[16,64,256]{2,1,0:T(8,128)(2,1)}), bf16[128,64,256]{2,1,0:T(8,128)(2,1)}) %all-gather.9.cloned.1.call-update) | async-done | bytes 4194320 | tf_op jit(solution)/shard_map/all_gather | solution.py:23
  195.6 4.8 %copy.41 = bf16[16,8,1,64,256]{4,3,1,0,2:T(8,128)(2,1)} copy(bf16[16,8,1,64,256]{4,3,0,1,2:T(8,128)(2,1)} %bitcast.70) | data formatting | bytes 8388608 | tf_op jit(solution)/shard_map/transpose | solution.py:27
  200.3 218.6 %while.18 = (s32[]{:T(128)}, f32[1,2,1024]{2,1,0:T(2,128)S(1)}, f32[1,2,1024]{2,1,0:T(2,128)S(1)}, f32[1,2,1024,128]{3,2,1,0:T(8,128)}, s32[8192]{0:T(1024)S(1)}...) while((s32[]{:T(128)}, f32[1,2,1024]{2,1,0:T(2,128)S(1)}, ...), condition=%wide.region_3.4_spmd.clone, body=%wide.region_0.3_spmd.clone.sunk | while | flops 276574464 | bytes 11423691 | solution.py:98
  201.4 1.0 constant_dynamic-slice_fusion.3
  203.3 2.1 fusion.33
  207.0 1.0 constant_dynamic-slice_fusion.3
  208.9 3.3 fusion.33
  215.8 3.3 fusion.33
  220.8 1.0 constant_dynamic-slice_fusion.3
  222.7 3.3 fusion.33
  227.6 1.0 constant_dynamic-slice_fusion.3
  229.5 3.3 fusion.33
  234.5 1.0 constant_dynamic-slice_fusion.3
  236.4 3.3 fusion.33
  241.4 1.0 constant_dynamic-slice_fusion.3
  243.3 3.3 fusion.33
  248.2 1.0 constant_dynamic-slice_fusion.3
  250.1 3.3 fusion.33
  255.1 1.0 constant_dynamic-slice_fusion.3
  257.0 3.3 fusion.33
  263.9 3.3 fusion.33
  270.8 3.3 fusion.33
  277.6 3.3 fusion.33
  284.5 3.3 fusion.33
  291.4 3.3 fusion.33
  298.2 3.3 fusion.33
  305.1 3.3 fusion.33
  312.0 3.3 fusion.33
  318.9 3.3 fusion.33
  325.7 3.3 fusion.33
  332.6 3.3 fusion.33
  339.5 3.3 fusion.33
  346.3 3.3 fusion.33
  353.2 3.3 fusion.33
  360.1 3.3 fusion.33
  367.0 3.3 fusion.33
  373.8 3.3 fusion.33
  380.7 3.3 fusion.33
  387.6 3.3 fusion.33
  394.4 3.3 fusion.33
  401.3 3.3 fusion.33
  408.2 3.3 fusion.33
  415.1 3.3 fusion.33
  419.0 1.6 broadcast_divide_fusion
  (397 shorter events, 106.6 us)
Async XLA Ops:
  6.5 105.6 %copy-start.1 = (s32[256]{0:T(256)S(1)}, s32[256]{0:T(256)}, u32[]{:S(2)}) copy-start(s32[256]{0:T(256)} %param.11) | copy-start | bytes 3076
  6.5 106.4 %copy-start = (bf16[1,64,4096]{2,1,0:T(8,128)(2,1)S(1)}, bf16[1,64,4096]{2,1,0:T(8,128)(2,1)}, u32[]{:S(2)}) copy-start(bf16[1,64,4096]{2,1,0:T(8,128)(2,1)} %param.7) | copy-start | bytes 1572868
  6.6 126.9 %all-gather.7.cloned.1.call-start = ((), (), s32[]{:S(2)}) async-start(), calls=%async_computation | async-start | bytes 4718592 | tf_op jit(solution)/shard_map/all_gather | solution.py:23
  80.3 115.3 %all-gather.9.cloned.1.call-start = ((), (), s32[]{:S(2)}) async-start(), calls=%async_computation.1 | async-start | bytes 4718592 | tf_op jit(solution)/shard_map/all_gather | solution.py:23
Sparse Core Ops, SparseCore 0:
  80.4 52.9 all-gather.6
  135.5 60.0 all-gather.8
where the time goes:
time: 433 us; the launch traced here: 429 us
  matrix products  125 us (29%)
  blocking collectives  105 us (24%)
  waiting for transfers between devices  77.4 us (18%)
  other arithmetic  53.3 us (12%)
  local copies, waits for them, and re-layouts  51.2 us (12%)
  between operations  14.2 us (3%)
    all_gather x2, blocking collectives, stacked_from(): pieces = lax.all_gather(pieces, axes[k], axis=0, tiled=True)  105 us
    dot_general x32, matrix products, attend(): jnp.einsum('shkr,skhd->shrd', weights.astype(jnp.bfloat16), value_four, p...  104 us
    all_gather x2, waiting for transfers between devices, stacked_from(): pieces = lax.all_gather(pieces, axes[k], axis=0, tiled=True)  77.2 us
    dynamic_slice x64, local copies, waits for them, and re-layouts, one_block(): lax.dynamic_slice_in_dim(value_rows, begin, size, 1)  34.9 us
    lt x32, other arithmetic, attend(): key_pos[None, :, None] < prompt_length[:, None, None]  23.3 us
    dot_general x32, matrix products, attend(): jnp.einsum('skhd,shdr->shkr', key_four, q_cols, preferred_element_type=jn...  20.8 us
    reduce_sum x32, other arithmetic, attend(): total = total * factor + jnp.sum(weights, axis=2)  18.2 us
    transpose x2, local copies, waits for them, and re-layouts, stacked_from(): pieces.transpose(*turned, *range(len(sequence), pieces.ndim))  9.46 us
  transfers between devices with their start and end apart: 2, of which 2 were waited for; matrix products, arithmetic and copies ran while one was open for 1% of the time, Pallas kernels for 0%

commit v1 on v0

v1 whole, which is shorter than its diff:
```python
import jax
import jax.numpy as jnp
from jax import lax
from jax.experimental import pallas as pl
from jax.experimental.pallas import tpu as pltpu
from jax.sharding import Mesh
from jax.sharding import PartitionSpec as P

HEAD_WIDTH = 128
BLK = ("blk_0", "blk_1")
BLOCK_SPANS = 16
NEG_FILL = -1e30
LOG2_E = 1.4426950408889634


def attend(table, q, gathered, local_heads, group, span):
    devices = gathered.shape[0]
    spans = devices * 2
    blocks = spans // BLOCK_SPANS
    keys_of = BLOCK_SPANS * span
    rows = group * span
    factor = LOG2_E * HEAD_WIDTH ** (-0.5)

    def kernel(table_ref, q_ref, kv_hbm, o_ref, kv_buf, s_buf, q_buf, m_buf, acc_buf, sems):
        limit = table_ref[spans + 2]

        def blocks_of(which):
            place = table_ref[spans + which]
            return jnp.where(place * span < limit, place // BLOCK_SPANS + 1, 0)

        most = jnp.maximum(blocks_of(0), blocks_of(1))

        def fetch(b, _):
            for i in range(BLOCK_SPANS):
                place = b * BLOCK_SPANS + i
                slot = table_ref[place]
                pltpu.make_async_copy(
                    kv_hbm.at[slot // 2, :, pl.ds(pl.multiple_of((slot % 2) * span, span), span), :],
                    kv_buf.at[:, pl.ds(pl.multiple_of(place * span, span), span), :],
                    sems.at[b],
                ).start()
            return 0

        lax.fori_loop(0, most, fetch, 0)

        def arrived(b):
            part = kv_buf.at[:, pl.ds(pl.multiple_of(b * keys_of, keys_of), keys_of), :]
            pltpu.make_async_copy(part, part, sems.at[b]).wait()

        def tile(t, _):
            head = t // 2
            which = t % 2
            place = table_ref[spans + which]
            count = blocks_of(which)
            row0 = pl.multiple_of(which * span, span)
            fresh = jnp.where(which == 0, 0, blocks_of(0))

            def columns(g):
                return pl.ds(pl.multiple_of((head * group + g) * HEAD_WIDTH, HEAD_WIDTH), HEAD_WIDTH)

            @pl.when(count == 0)
            def _():
                for g in range(group):
                    o_ref[pl.ds(row0, span), columns(g)] = jnp.zeros((span, HEAD_WIDTH), o_ref.dtype)

            @pl.when(count > 0)
            def _():
                for g in range(group):
                    q_buf[g * span : (g + 1) * span, :] = q_ref[pl.ds(row0, span), columns(g)]
                m_buf[...] = jnp.full(m_buf.shape, NEG_FILL, jnp.float32)
                acc_buf[...] = jnp.zeros(acc_buf.shape, jnp.float32)

                def score(b, masked):
                    @pl.when((head == 0) & (b >= fresh))
                    def _():
                        arrived(b)

                    part = kv_buf[head, pl.ds(pl.multiple_of(b * keys_of, keys_of), keys_of), :]
                    s = lax.dot_general(
                        q_buf[...], part, (((1,), (1,)), ((), ())), preferred_element_type=jnp.float32
                    )
                    if masked:
                        key_pos = b * keys_of + lax.broadcasted_iota(jnp.int32, s.shape, 1)
                        row_pos = place * span + lax.broadcasted_iota(jnp.int32, s.shape, 0) % span
                        s = jnp.where(key_pos <= row_pos, s, NEG_FILL)
                    s_buf[b] = s
                    top = m_buf[...]
                    for c in range(keys_of // 128):
                        top = jnp.maximum(top, s[:, c * 128 : (c + 1) * 128])
                    m_buf[...] = top

                def plain(b, _):
                    score(b, False)
                    return 0

                lax.fori_loop(0, count - 1, plain, 0)
                score(count - 1, True)
                m_buf[...] = jnp.broadcast_to(jnp.max(m_buf[...], axis=1, keepdims=True), m_buf.shape)

                def mix(b, _):
                    top = jnp.concatenate([m_buf[...]] * (keys_of // 128), axis=1)
                    w = jnp.exp2((s_buf[b] - top) * factor).astype(jnp.bfloat16)
                    v = kv_buf[local_heads + head, pl.ds(pl.multiple_of(b * keys_of, keys_of), keys_of), :]
                    wide = jnp.concatenate([v, jnp.ones_like(v)], axis=1)
                    acc_buf[...] += jnp.dot(w, wide, preferred_element_type=jnp.float32)
                    return 0

                lax.fori_loop(0, count, mix, 0)
                out = acc_buf[:, :HEAD_WIDTH] / acc_buf[:, HEAD_WIDTH:]
                row_pos = place * span + lax.broadcasted_iota(jnp.int32, out.shape, 0) % span
                out = jnp.where(row_pos < limit, out, 0.0).astype(o_ref.dtype)
                for g in range(group):
                    o_ref[pl.ds(row0, span), columns(g)] = out[g * span : (g + 1) * span]

            return 0

        lax.fori_loop(0, 2 * local_heads, tile, 0)

    return pl.pallas_call(
        kernel,
        out_shape=jax.ShapeDtypeStruct(q.shape, q.dtype),
        in_specs=[
            pl.BlockSpec(memory_space=pltpu.SMEM),
            pl.BlockSpec(memory_space=pltpu.VMEM),
            pl.BlockSpec(memory_space=pl.ANY),
        ],
        out_specs=pl.BlockSpec(memory_space=pltpu.VMEM),
        scratch_shapes=[
            pltpu.VMEM((2 * local_heads, spans * span, HEAD_WIDTH), jnp.bfloat16),
            pltpu.VMEM((blocks, rows, keys_of), jnp.float32),
            pltpu.VMEM((rows, HEAD_WIDTH), jnp.bfloat16),
            pltpu.VMEM((rows, 128), jnp.float32),
            pltpu.VMEM((rows, 2 * HEAD_WIDTH), jnp.float32),
            pltpu.SemaphoreType.DMA((blocks,)),
        ],
        compiler_params=pltpu.CompilerParams(vmem_limit_bytes=48 * 1024 * 1024),
    )(table, q, gathered)


def shards(queries, keys, values, prompt_length, span_order):
    mine = lax.axis_index(BLK)
    tok_rows = queries.shape[1]
    span = tok_rows // 2
    local_heads = keys.shape[2] // HEAD_WIDTH
    group = queries.shape[2] // (local_heads * HEAD_WIDTH)
    spans = span_order.shape[0]
    every = jnp.arange(spans, dtype=jnp.int32)
    slot_of = jnp.sum(jnp.where(span_order[None, :] == every[:, None], every[None, :], 0), axis=1)
    table = jnp.concatenate(
        [slot_of, lax.dynamic_slice_in_dim(span_order, mine * 2, 2), prompt_length]
    ).astype(jnp.int32)
    pieces = [keys[0, :, h * HEAD_WIDTH : (h + 1) * HEAD_WIDTH] for h in range(local_heads)]
    pieces += [values[0, :, h * HEAD_WIDTH : (h + 1) * HEAD_WIDTH] for h in range(local_heads)]
    packed = jnp.stack(pieces)
    gathered = lax.all_gather(packed, BLK, axis=0, tiled=False)
    return attend(table, queries[0], gathered, local_heads, group, span)[None]


def solution(mesh):
    blk = mesh.shape["blk"]
    split = Mesh(
        mesh.devices.reshape(mesh.shape["rep"], blk // 8, 8, mesh.shape["head"]),
        ("rep", "blk_0", "blk_1", "head"),
    )
    in_specs = (
        P("rep", BLK, "head"),
        P("rep", BLK, "head"),
        P("rep", BLK, "head"),
        P("rep"),
        P("rep"),
    )
    out_specs = P("rep", BLK, "head")
    return jax.shard_map(
        shards, mesh=split, in_specs=in_specs, out_specs=out_specs, check_vma=False
    )
```

time: 433 us -> 238 us (0.55); the launches traced: 429 us -> 241 us
  matrix products: 125 us -> 0 us
  waiting for transfers between devices: 77.4 us -> 186 us
  blocking collectives: 105 us -> 0 us
  other arithmetic: 53.3 us -> 1.51 us
  local copies, waits for them, and re-layouts: 51.2 us -> 2.57 us
  Pallas kernels: 0 us -> 36.4 us
    dot_general x64 -> x0, matrix products: 125 us -> none  [the longest x32 104 us: attend(): jnp.einsum('shkr,skhd->shrd', weights.astype(jnp.bfloat16), value_four, p...]
    all_gather x2 -> x1, waiting for transfers between devices: 77.2 us -> 186 us  [shards(): gathered = lax.all_gather(packed, BLK, axis=0, tiled=False)]
    all_gather x2 -> x0, blocking collectives: 105 us -> none  [stacked_from(): pieces = lax.all_gather(pieces, axes[k], axis=0, tiled=True)]
    dynamic_slice x96 -> x1, local copies, waits for them, and re-layouts: 38.1 us -> 0.76 us  [shards(): lax.dynamic_slice_in_dim(span_order, mine * 2, 2)]
    pallas_call x0 -> x1, Pallas kernels: none -> 36.4 us  [attend(): pl.pallas_call(kernel, out_shape=jax.ShapeDtypeStruct(q.shape, q.dtype),...]
    lt x33 -> x0, other arithmetic: 23.3 us -> none  [the longest x32 23.3 us: attend(): key_pos[None, :, None] < prompt_length[:, None, None]]
    reduce_sum x32 -> x1, other arithmetic: 18.2 us -> 0.79 us  [shards(): jnp.sum(jnp.where(span_order[None, :] == every[:, None], every[None, :],...]
    transpose x3 -> x0, local copies, waits for them, and re-layouts: 9.67 us -> none  [the longest x2 9.46 us: stacked_from(): pieces.transpose(*turned, *range(len(sequence), pieces.ndim))]
  transfers between devices with their start and end apart: 2 -> 1, of which waited for: 2 -> 1; matrix products, arithmetic and copies ran while one was open for 1% -> 1% of each run, Pallas kernels for 0% -> 0%
where the time goes in v1:
time: 238 us; the launch traced here: 241 us
  waiting for transfers between devices  186 us (78%)
  Pallas kernels  36.4 us (15%)
  between operations  14.1 us (6%)
  local copies, waits for them, and re-layouts  2.57 us (1%)
    all_gather x1, waiting for transfers between devices, shards(): gathered = lax.all_gather(packed, BLK, axis=0, tiled=False)  186 us
    pallas_call x1, Pallas kernels, attend(): pl.pallas_call(kernel, out_shape=jax.ShapeDtypeStruct(q.shape, q.dtype),...  36.4 us
  transfers between devices with their start and end apart: 1, of which 1 were waited for; matrix products, arithmetic and copies ran while one was open for 1% of the time, Pallas kernels for 0%

profile of v1, /device:TPU:80, one launch (start us, length us, event | category | flops | bytes accessed | tf_op | source)
XLA Modules:
  0.0 240.9 jit_solution(4266597435846192367)
XLA Ops:
  6.5 0.0 all-gather.3.cloned.1.call-start
  6.6 0.8 fusion
  7.3 0.6 pad_maximum_fusion
  8.0 0.1 all-gather.3.cloned.1.call-update
  8.7 0.8 dynamic_slice.3
  9.4 0.8 select_reduce_fusion
  10.2 0.1 pad_add_fusion.table_ref
  10.3 186.2 %all-gather.3.cloned.1.call-done = bf16[512,64,128]{2,1,0:T(8,128)(2,1)} async-done(((bf16[4,64,128]{2,1,0:T(8,128)(2,1)}), bf16[512,64,128]{2,1,0:T(8,128)(2,1)}) %all-gather.3.cloned.1.call-update) | async-done | bytes 8388624 | tf_op jit(solution)/shard_map/all_gather | solution.py:155
  196.5 0.0 copy-start
  196.5 1.0 copy-done
  197.6 36.4 %shard_map.55 = bf16[64,4096]{1,0:T(8,128)(2,1)} custom-call(s32[259]{0:T(512)S(1)} %pad_add_fusion.table_ref, bf16[64,4096]{1,0:T(8,128)(2,1)S(1)} %bitcast.3, bf16[128,4,64,128]{3,2,1,0:T(8,128)(2,1)} %bitcast.4), custom_call_target="tpu_custom_call" | custom-call | tf_op jit(solution)/shard_map/pallas_call | solution.py:119
Async XLA Ops:
  6.5 190.0 %all-gather.3.cloned.1.call-start = ((), (), s32[]{:S(2)}) async-start(), calls=%async_computation | async-start | bytes 8454144 | tf_op jit(solution)/shard_map/all_gather | solution.py:155
  196.5 1.0 copy-start
Sparse Core Ops, SparseCore 0:
  10.3 186.1 all-gather.2
